TPU v7x, 32 devices: a 4x2x2 block of a 4x4x8 slice. The times are simulated.
32 devices in a mesh: replica: 4 (over y, z), dp: 8 (over x, core).
Axes of the slice: x: 4, y: 2, z: 2, core: 2. Of those that a mesh axis runs over, the one named last changes fastest.
The devices are a block of a 4x4x8 slice.
Arguments:
- x: bfloat16 [2048, 896], P(('replica', 'dp')), parts along dimension 0
- lengths: int32 [2048], P(('replica', 'dp')), parts along dimension 0
- cache: bfloat16 [2, 2048, 64, 576], P(None, ('replica', 'dp')), parts along dimension 1
- w_q: bfloat16 [2, 896, 4608], replicated
- w_o: bfloat16 [2, 4096, 896], replicated
- expert_ids: int32 [2, 2048, 8], P(None, ('replica', 'dp')), parts along dimension 1
- slots: int32 [2, 2048, 8], P(None, ('replica', 'dp')), parts along dimension 1
- route_w: float32 [2, 2048, 8], P(None, ('replica', 'dp')), parts along dimension 1
- w1_exp: bfloat16 [2, 384, 896, 256], P(None, 'dp')
- w3_exp: bfloat16 [2, 384, 896, 256], P(None, 'dp')
- w2_exp: bfloat16 [2, 384, 256, 896], P(None, 'dp')
- w1_sh: bfloat16 [2, 896, 256], P(None, None, 'dp')
- w3_sh: bfloat16 [2, 896, 256], P(None, None, 'dp')
- w2_sh: bfloat16 [2, 256, 896], P(None, 'dp')
Outputs:
- output: bfloat16 [2048, 896], P(('replica', 'dp')), parts along dimension 0
There are 4 independent parts. A program takes and returns all parts, laid end to end along the dimension named above; an argument that names none is the same for every part.
All inputs are finite; a program needn't handle non-finite values.
Results may differ from a plain program's by a relative error of at most 0.02.
Values are sent between devices in bfloat16 or wider.
A program may use at most 768 MiB of HBM per device.

v0:
```python
import jax
import jax.numpy as jnp
from jax import lax
from jax.sharding import PartitionSpec as P

NORM_EPS = 1e-6
ATT_SCALE = 1.0 / (192.0 ** 0.5)
LATENT = 512


def rms_norm(values):
    vals32 = values.astype(jnp.float32)
    return vals32 * lax.rsqrt(jnp.mean(vals32 * vals32, axis=-1, keepdims=True) + NORM_EPS)


def gated_hidden(tok_in, w_up, w_gate):
    gate_in = jnp.dot(tok_in, w_gate, preferred_element_type=jnp.float32)
    up_in = jnp.dot(tok_in, w_up, preferred_element_type=jnp.float32)
    return (jax.nn.silu(gate_in) * up_in).astype(jnp.bfloat16)


def local_attention(resid, lengths, cache_l, w_q_l, w_o_l):
    tok_count = resid.shape[0]
    seq_len, kv_dim = cache_l.shape[1], cache_l.shape[2]
    num_heads = w_q_l.shape[1] // kv_dim
    normed = rms_norm(resid).astype(jnp.bfloat16)
    queries = jnp.dot(normed, w_q_l, preferred_element_type=jnp.float32).astype(jnp.bfloat16)
    queries = queries.reshape(tok_count, num_heads, kv_dim)
    scores = jnp.einsum('bhc,btc->bht', queries, cache_l, preferred_element_type=jnp.float32) * ATT_SCALE
    valid = jnp.arange(seq_len)[None, None, :] < lengths[:, None, None]
    probs = jax.nn.softmax(jnp.where(valid, scores, -jnp.inf), axis=-1).astype(jnp.bfloat16)
    attn = jnp.einsum('bht,btc->bhc', probs, cache_l[:, :, :LATENT], preferred_element_type=jnp.float32)
    attn = attn.astype(jnp.bfloat16).reshape(tok_count, num_heads * LATENT)
    return (resid.astype(jnp.float32) + jnp.dot(attn, w_o_l, preferred_element_type=jnp.float32)).astype(jnp.bfloat16)


def route_select(ids_l, slot_l, experts, capacity):
    buf_rows = jnp.where(slot_l >= 0, ids_l * capacity + slot_l, -1)
    return (buf_rows[:, :, None] == jnp.arange(experts * capacity)).astype(jnp.bfloat16)


def solution(mesh):
    group = mesh.shape['dp']
    tok_axes = ('replica', 'dp')
    in_specs = (
        P(tok_axes, None), P(tok_axes), P(None, tok_axes, None, None),
        P(None, None, None), P(None, None, None),
        P(None, tok_axes, None), P(None, tok_axes, None), P(None, tok_axes, None),
        P(None, 'dp', None, None), P(None, 'dp', None, None), P(None, 'dp', None, None),
        P(None, None, 'dp'), P(None, None, 'dp'), P(None, 'dp', None),
    )

    def device_step(x, lengths, cache, w_q, w_o, expert_ids, slots, route_w, w1_exp, w3_exp, w2_exp, w1_sh, w3_sh, w2_sh):
        batch_dev, d_model = x.shape
        local_experts = w1_exp.shape[1]
        experts = local_experts * group
        top_k = expert_ids.shape[2]
        capacity = max(1, (2 * batch_dev * top_k) // experts)
        resid = x
        for layer_idx in range(cache.shape[0]):
            resid = local_attention(resid, lengths, cache[layer_idx], w_q[layer_idx], w_o[layer_idx])
            ffn_in = rms_norm(resid).astype(jnp.bfloat16)
            gathered = lax.all_gather(ffn_in, 'dp', axis=0, tiled=True)
            shared_h = gated_hidden(gathered, w1_sh[layer_idx], w3_sh[layer_idx])
            shared_part = jnp.dot(shared_h, w2_sh[layer_idx], preferred_element_type=jnp.float32)
            shared_out = lax.psum_scatter(shared_part, 'dp', scatter_dimension=0, tiled=True)
            select = route_select(expert_ids[layer_idx], slots[layer_idx], experts, capacity)
            dispatch = jnp.sum(select, axis=1)
            send_buf = jnp.einsum('br,bd->rd', dispatch, ffn_in, preferred_element_type=jnp.float32).astype(jnp.bfloat16)
            send_buf = send_buf.reshape(group, local_experts, capacity, d_model)
            recv_buf = lax.all_to_all(send_buf, 'dp', 0, 0, tiled=True)
            gate_in = jnp.einsum('sncd,ndf->nscf', recv_buf, w3_exp[layer_idx], preferred_element_type=jnp.float32)
            up_in = jnp.einsum('sncd,ndf->nscf', recv_buf, w1_exp[layer_idx], preferred_element_type=jnp.float32)
            hidden = (jax.nn.silu(gate_in) * up_in).astype(jnp.bfloat16)
            expert_out = jnp.einsum('nscf,nfd->sncd', hidden, w2_exp[layer_idx], preferred_element_type=jnp.float32).astype(jnp.bfloat16)
            returned = lax.all_to_all(expert_out, 'dp', 0, 0, tiled=True)
            returned = returned.reshape(experts * capacity, d_model)
            picked = jnp.einsum('cls,se->cle', select, returned, preferred_element_type=jnp.float32)
            routed = jnp.sum(route_w[layer_idx][:, :, None] * picked, axis=1)
            resid = (resid.astype(jnp.float32) + routed + shared_out).astype(jnp.bfloat16)
        return resid

    return jax.shard_map(device_step, mesh=mesh, in_specs=in_specs, out_specs=P(tok_axes, None), check_vma=False)
```

profile of v0, /device:TPU:81, one launch (start us, length us, event | category | flops | bytes accessed | tf_op | source)
XLA Modules:
  0.0 239.9 jit_solution(16784056383840485202)
XLA Ops:
  8.3 5.0 %fusion.32 = bf16[64,4608]{1,0:T(8,128)(2,1)S(1)} fusion(bf16[2,896,4608]{2,1,0:T(8,128)(2,1)} %param.17, bf16[64,896]{1,0:T(8,128)(2,1)} %param.14, f32[64]{0:T(128)S(1)} %add_rsqrt_fusion.3), kind=kOutput, calls=%fused_computation.32 | convolution fusion | flops 528949248 | bytes 8962304 | tf_op jit(solution)/shard_map/dot_general | solution.py:27
  13.9 9.0 %slice_bitcast_fusion.1 = (bf16[64,64,576]{2,1,0:T(8,128)(2,1)}, bf16[64,64,576]{2,1,0:T(8,128)(2,1)}) fusion(bf16[2,64,64,576]{3,2,1,0:T(8,128)(2,1)} %param.16), kind=kLoop, calls=%fused_computation.35 | loop fusion | bytes 18874368 | tf_op jit(solution)/shard_map/squeeze | solution.py:61
  22.8 4.4 %fusion.184 = (f32[64,8]{1,0:T(8,128)S(1)}, f32[64,8,64]{2,1,0:T(8,128)S(1)}) fusion(bf16[64,8,576]{2,1,0:T(8,128)(2,1)S(1)} %reshape.127, pred[64,64]{1,0:T(8,128)(4,1)S(1)} %iota_compare_fusion.8, bf16[2,64,64,576]{3,2,1,0:T(8,128)(2,1)} %param.16), kind=kOutput, calls=%fused_computation.159 | convolution fusion | flops 37879872 | bytes 5969920 | tf_op jit(solution)/shard_map/sub | solution.py:31
  27.2 2.9 %fusion.58 = bf16[64,8,512]{2,1,0:T(8,128)(2,1)S(1)} fusion(bf16[64,64,576]{2,1,0:T(8,128)(2,1)} %get-tuple-element.7, f32[64,8,64]{2,1,0:T(8,128)S(1)} %get-tuple-element.14, f32[64,8]{1,0:T(8,128)S(1)} %get-tuple-element.13), kind=kOutput, calls=%fused_computation.54 | convolution fusion | flops 33882112 | bytes 4851712 | tf_op jit(solution)/shard_map/bht,btc->bhc/dot_general | solution.py:32
  30.4 4.4 %multiply_reduce_fusion.3 = (f32[64]{0:T(128)S(1)}, f32[64,896]{1,0:T(8,128)S(1)}) fusion(bf16[64,4096]{1,0:T(8,128)(2,1)S(1)} %bitcast.150, bf16[2,4096,896]{2,1,0:T(8,128)(2,1)} %param.18, bf16[64,896]{1,0:T(8,128)(2,1)S(1)} %copy-done.8), kind=kOutput, calls=%fused_computation.115 | convolution fusion | flops 470106048 | bytes 8208640 | tf_op jit(solution)/shard_map/dot_general | solution.py:34
  37.7 6.0 %all-to-all-start = ((bf16[8,48,2,896]{3,2,1,0:T(2,128)(2,1)}), bf16[8,48,2,896]{3,2,1,0:T(2,128)(2,1)S(1)}, u32[]{:S(2)}, u32[]{:S(2)}) async-start(bf16[8,48,2,896]{3,2,1,0:T(2,128)(2,1)} %reshape.129), calls=%async_computation | async-start | bytes 2752512 | tf_op jit(solution)/shard_map/all_to_all | solution.py:71
  43.7 27.6 %all_gather.6 = bf16[512,896]{1,0:T(8,128)(2,1)S(1)} all-gather(bf16[64,896]{1,0:T(8,128)(2,1)S(1)} %multiply_convert_fusion.1), channel_id=1, replica_groups=mesh['replica'=4,'dp'=8] {'dp'}, dimensions={0}, use_global_device_ids=true | all-gather | bytes 1032192 | tf_op jit(solution)/shard_map/all_gather | solution.py:63
  71.7 2.1 fusion.123
  73.8 8.8 %fusion.12 = f32[48,8,2,256]{3,1,2,0:T(8,128)S(1)} fusion(bf16[2,48,896,256]{3,2,1,0:T(8,128)(2,1)} %param.23, bf16[8,48,2,896]{3,2,1,0:T(2,128)(2,1)S(1)} %all-to-all-done), kind=kOutput, calls=%fused_computation.12 | convolution fusion | flops 352321536 | bytes 24182784 | tf_op jit(solution)/shard_map/sncd,ndf->nscf/dot_general | solution.py:72
  82.6 15.8 %fusion.55 = bf16[8,48,2,896]{3,0,2,1:T(8,128)(2,1)S(1)} fusion(bf16[2,48,256,896]{3,2,1,0:T(8,128)(2,1)} %param.24, bf16[2,48,896,256]{3,2,1,0:T(8,128)(2,1)} %param.22, bf16[8,48,2,896]{3,2,1,0:T(2,128)(2,1)S(1)} %all-to-all-done, f32[48,8,2,256]{3,1,2,0:T(8,128)S(1)} %fusion.12), kind=kOutput, calls=%fused_computation.53 | convolution fusion | flops 706510848 | bytes 47579136 | tf_op jit(solution)/shard_map/nscf,nfd->sncd/dot_general | solution.py:75
  98.5 2.2 copy.33
  100.6 4.0 %all-to-all-start.1 = ((bf16[8,48,2,896]{3,2,1,0:T(2,128)(2,1)}), bf16[8,48,2,896]{3,2,1,0:T(2,128)(2,1)S(1)}, u32[]{:S(2)}, u32[]{:S(2)}) async-start(bf16[8,48,2,896]{3,2,1,0:T(2,128)(2,1)} %copy.33), calls=%async_computation.1 | async-start | bytes 2752512 | tf_op jit(solution)/shard_map/all_to_all | solution.py:76
  105.5 17.3 %all-to-all-done.1 = bf16[8,48,2,896]{3,2,1,0:T(2,128)(2,1)S(1)} async-done(((bf16[8,48,2,896]{3,2,1,0:T(2,128)(2,1)}), bf16[8,48,2,896]{3,2,1,0:T(2,128)(2,1)S(1)}, u32[]{:S(2)}, u32[]{:S(2)}) %all-to-all-start.1) | async-done | bytes 1376288 | tf_op jit(solution)/shard_map/all_to_all | solution.py:76
  125.7 5.0 %fusion.35 = bf16[64,4608]{1,0:T(8,128)(2,1)S(1)} fusion(bf16[2,896,4608]{2,1,0:T(8,128)(2,1)} %param.17, bf16[64,896]{1,0:T(8,128)(2,1)S(1)} %get-tuple-element.6, f32[64]{0:T(128)S(1)} %add_rsqrt_fusion.1), kind=kOutput, calls=%fused_computation.33 | convolution fusion | flops 528949248 | bytes 8962304 | tf_op jit(solution)/shard_map/dot_general | solution.py:27
  131.2 4.4 %fusion.185 = (f32[64,8]{1,0:T(8,128)S(1)}, f32[64,8,64]{2,1,0:T(8,128)S(1)}) fusion(bf16[64,8,576]{2,1,0:T(8,128)(2,1)S(1)} %reshape.131, pred[64,64]{1,0:T(8,128)(4,1)S(1)} %iota_compare_fusion.8, bf16[2,64,64,576]{3,2,1,0:T(8,128)(2,1)} %param.16), kind=kOutput, calls=%fused_computation.160 | convolution fusion | flops 37879872 | bytes 5969920 | tf_op jit(solution)/shard_map/sub | solution.py:31
  135.6 2.9 %fusion.61 = bf16[64,8,512]{2,1,0:T(8,128)(2,1)S(1)} fusion(bf16[64,64,576]{2,1,0:T(8,128)(2,1)} %get-tuple-element.8, f32[64,8,64]{2,1,0:T(8,128)S(1)} %get-tuple-element.18, f32[64,8]{1,0:T(8,128)S(1)} %get-tuple-element.17), kind=kOutput, calls=%fused_computation.55 | convolution fusion | flops 33882112 | bytes 4851712 | tf_op jit(solution)/shard_map/bht,btc->bhc/dot_general | solution.py:32
  138.6 4.4 %multiply_reduce_fusion.2 = (f32[64]{0:T(128)S(1)}, f32[64,896]{1,0:T(8,128)S(1)}) fusion(bf16[64,4096]{1,0:T(8,128)(2,1)S(1)} %bitcast.148, bf16[2,4096,896]{2,1,0:T(8,128)(2,1)} %param.18, bf16[64,896]{1,0:T(8,128)(2,1)S(1)} %get-tuple-element.6), kind=kOutput, calls=%fused_computation.112 | convolution fusion | flops 470106048 | bytes 8208640 | tf_op jit(solution)/shard_map/dot_general | solution.py:34
  145.9 4.7 %all-to-all-start.2 = ((bf16[8,48,2,896]{3,2,1,0:T(2,128)(2,1)}), bf16[8,48,2,896]{3,2,1,0:T(2,128)(2,1)S(1)}, u32[]{:S(2)}, u32[]{:S(2)}) async-start(bf16[8,48,2,896]{3,2,1,0:T(2,128)(2,1)} %reshape.133), calls=%async_computation.3 | async-start | bytes 2752512 | tf_op jit(solution)/shard_map/all_to_all | solution.py:71
  150.5 27.7 %all_gather.7 = bf16[512,896]{1,0:T(8,128)(2,1)S(1)} all-gather(bf16[64,896]{1,0:T(8,128)(2,1)S(1)} %multiply_convert_fusion), channel_id=1, replica_groups=mesh['replica'=4,'dp'=8] {'dp'}, dimensions={0}, use_global_device_ids=true | all-gather | bytes 1032192 | tf_op jit(solution)/shard_map/all_gather | solution.py:63
  180.7 8.8 %fusion.6 = f32[48,8,2,256]{3,1,2,0:T(8,128)S(1)} fusion(bf16[2,48,896,256]{3,2,1,0:T(8,128)(2,1)} %param.23, bf16[8,48,2,896]{3,2,1,0:T(2,128)(2,1)S(1)} %all-to-all-done.2), kind=kOutput, calls=%fused_computation.6 | convolution fusion | flops 352321536 | bytes 24182784 | tf_op jit(solution)/shard_map/sncd,ndf->nscf/dot_general | solution.py:72
  189.5 15.8 %fusion.52 = bf16[8,48,2,896]{3,0,2,1:T(8,128)(2,1)S(1)} fusion(bf16[2,48,256,896]{3,2,1,0:T(8,128)(2,1)} %param.24, bf16[2,48,896,256]{3,2,1,0:T(8,128)(2,1)} %param.22, bf16[8,48,2,896]{3,2,1,0:T(2,128)(2,1)S(1)} %all-to-all-done.2, f32[48,8,2,256]{3,1,2,0:T(8,128)S(1)} %fusion.6), kind=kOutput, calls=%fused_computation.52 | convolution fusion | flops 706510848 | bytes 47579136 | tf_op jit(solution)/shard_map/nscf,nfd->sncd/dot_general | solution.py:75
  205.3 2.2 copy.38
  207.5 3.8 %all-to-all-start.3 = ((bf16[8,48,2,896]{3,2,1,0:T(2,128)(2,1)}), bf16[8,48,2,896]{3,2,1,0:T(2,128)(2,1)S(1)}, u32[]{:S(2)}, u32[]{:S(2)}) async-start(bf16[8,48,2,896]{3,2,1,0:T(2,128)(2,1)} %copy.38), calls=%async_computation.4 | async-start | bytes 2752512 | tf_op jit(solution)/shard_map/all_to_all | solution.py:76
  211.4 18.3 %all-to-all-done.3 = bf16[8,48,2,896]{3,2,1,0:T(2,128)(2,1)S(1)} async-done(((bf16[8,48,2,896]{3,2,1,0:T(2,128)(2,1)}), bf16[8,48,2,896]{3,2,1,0:T(2,128)(2,1)S(1)}, u32[]{:S(2)}, u32[]{:S(2)}) %all-to-all-start.3) | async-done | bytes 1376288 | tf_op jit(solution)/shard_map/all_to_all | solution.py:76
  (77 shorter events, 18.7 us)
Async XLA Ops:
  27.2 3.1 %copy-start.8 = (bf16[64,896]{1,0:T(8,128)(2,1)S(1)}, bf16[64,896]{1,0:T(8,128)(2,1)}, u32[]{:S(2)}) copy-start(bf16[64,896]{1,0:T(8,128)(2,1)} %param.14) | copy-start | bytes 344068
  30.4 4.5 %copy-start.15 = (s32[2,64,8]{1,2,0:T(8,128)S(1)}, s32[2,64,8]{1,2,0:T(8,128)}, u32[]{:S(2)}) copy-start(s32[2,64,8]{1,2,0:T(8,128)} %param.19) | copy-start | bytes 12292
  30.4 4.5 %copy-start.16 = (s32[2,64,8]{1,2,0:T(8,128)S(1)}, s32[2,64,8]{1,2,0:T(8,128)}, u32[]{:S(2)}) copy-start(s32[2,64,8]{1,2,0:T(8,128)} %param.20) | copy-start | bytes 12292
  34.8 0.7 copy-start
  35.0 0.6 copy-start.6
  35.6 35.7 %copy-start.9 = (bf16[2,896,32]{1,2,0:T(8,128)(2,1)S(1)}, bf16[2,896,32]{1,2,0:T(8,128)(2,1)}, u32[]{:S(2)}) copy-start(bf16[2,896,32]{1,2,0:T(8,128)(2,1)} %param.26) | copy-start | bytes 344068
  35.7 36.0 %copy-start.11 = (bf16[2,32,896]{2,1,0:T(8,128)(2,1)S(1)}, bf16[2,32,896]{2,1,0:T(8,128)(2,1)}, u32[]{:S(2)}) copy-start(bf16[2,32,896]{2,1,0:T(8,128)(2,1)} %param.27) | copy-start | bytes 344068
  35.7 36.0 %copy-start.13 = (bf16[2,896,32]{1,2,0:T(8,128)(2,1)S(1)}, bf16[2,896,32]{1,2,0:T(8,128)(2,1)}, u32[]{:S(2)}) copy-start(bf16[2,896,32]{1,2,0:T(8,128)(2,1)} %param.25) | copy-start | bytes 344068
  37.7 36.1 %all-to-all-start = ((bf16[8,48,2,896]{3,2,1,0:T(2,128)(2,1)}), bf16[8,48,2,896]{3,2,1,0:T(2,128)(2,1)S(1)}, u32[]{:S(2)}, u32[]{:S(2)}) async-start(bf16[8,48,2,896]{3,2,1,0:T(2,128)(2,1)} %reshape.129), calls=%async_computation | async-start | bytes 2752512 | tf_op jit(solution)/shard_map/all_to_all | solution.py:71
  43.7 80.9 %reduce-scatter.3.cloned.1.call-start = ((), (), s32[]{:S(2)}) async-start(), calls=%async_computation.6 | async-start | bytes 2064384 | tf_op jit(solution)/shard_map/reduce_scatter | solution.py:66
  98.5 6.2 %copy-start.17 = (f32[2,64,8]{1,2,0:T(8,128)S(1)}, f32[2,64,8]{1,2,0:T(8,128)}, u32[]{:S(2)}) copy-start(f32[2,64,8]{1,2,0:T(8,128)} %param.21) | copy-start | bytes 12292
  100.6 22.7 %copy-start.7 = (s32[64,8]{1,0:T(8,128)S(1)}, s32[64,8]{1,0:T(8,128)}, u32[]{:S(2)}) copy-start(s32[64,8]{1,0:T(8,128)} %copy-done.6) | copy-start | bytes 6148
  100.6 22.1 %all-to-all-start.1 = ((bf16[8,48,2,896]{3,2,1,0:T(2,128)(2,1)}), bf16[8,48,2,896]{3,2,1,0:T(2,128)(2,1)S(1)}, u32[]{:S(2)}, u32[]{:S(2)}) async-start(bf16[8,48,2,896]{3,2,1,0:T(2,128)(2,1)} %copy.33), calls=%async_computation.1 | async-start | bytes 2752512 | tf_op jit(solution)/shard_map/all_to_all | solution.py:76
  104.7 19.9 %copy-start.1 = (f32[64,896]{1,0:T(8,128)S(1)}, f32[64,896]{1,0:T(8,128)}, u32[]{:S(2)}) copy-start(f32[64,896]{1,0:T(8,128)} %copy-done) | copy-start | bytes 688132
  104.9 0.6 copy-start.4
  143.1 0.7 copy-start.2
  143.8 34.4 %copy-start.10 = (bf16[2,896,32]{1,2,0:T(8,128)(2,1)S(1)}, bf16[2,896,32]{1,2,0:T(8,128)(2,1)}, u32[]{:S(2)}) copy-start(bf16[2,896,32]{1,2,0:T(8,128)(2,1)} %param.26) | copy-start | bytes 344068
  143.9 34.7 %copy-start.12 = (bf16[2,32,896]{2,1,0:T(8,128)(2,1)S(1)}, bf16[2,32,896]{2,1,0:T(8,128)(2,1)}, u32[]{:S(2)}) copy-start(bf16[2,32,896]{2,1,0:T(8,128)(2,1)} %param.27) | copy-start | bytes 344068
  143.9 34.7 %copy-start.14 = (bf16[2,896,32]{1,2,0:T(8,128)(2,1)S(1)}, bf16[2,896,32]{1,2,0:T(8,128)(2,1)}, u32[]{:S(2)}) copy-start(bf16[2,896,32]{1,2,0:T(8,128)(2,1)} %param.25) | copy-start | bytes 344068
  145.9 34.8 %all-to-all-start.2 = ((bf16[8,48,2,896]{3,2,1,0:T(2,128)(2,1)}), bf16[8,48,2,896]{3,2,1,0:T(2,128)(2,1)S(1)}, u32[]{:S(2)}, u32[]{:S(2)}) async-start(bf16[8,48,2,896]{3,2,1,0:T(2,128)(2,1)} %reshape.133), calls=%async_computation.3 | async-start | bytes 2752512 | tf_op jit(solution)/shard_map/all_to_all | solution.py:71
  150.5 80.9 %reduce-scatter.5.cloned.1.call-start = ((), (), s32[]{:S(2)}) async-start(), calls=%async_computation.7 | async-start | bytes 2064384 | tf_op jit(solution)/shard_map/reduce_scatter | solution.py:66
  207.5 22.7 %copy-start.5 = (s32[64,8]{1,0:T(8,128)S(1)}, s32[64,8]{1,0:T(8,128)}, u32[]{:S(2)}) copy-start(s32[64,8]{1,0:T(8,128)} %copy-done.4) | copy-start | bytes 6148
  207.5 22.1 %all-to-all-start.3 = ((bf16[8,48,2,896]{3,2,1,0:T(2,128)(2,1)}), bf16[8,48,2,896]{3,2,1,0:T(2,128)(2,1)S(1)}, u32[]{:S(2)}, u32[]{:S(2)}) async-start(bf16[8,48,2,896]{3,2,1,0:T(2,128)(2,1)} %copy.38), calls=%async_computation.4 | async-start | bytes 2752512 | tf_op jit(solution)/shard_map/all_to_all | solution.py:76
  211.3 20.1 %copy-start.3 = (f32[64,896]{1,0:T(8,128)S(1)}, f32[64,896]{1,0:T(8,128)}, u32[]{:S(2)}) copy-start(f32[64,896]{1,0:T(8,128)} %copy-done.2) | copy-start | bytes 688132
Sparse Core Ops, SparseCore 0:
  73.9 28.3 reduce-scatter.2
  180.8 28.3 reduce-scatter.4
where the time goes:
time: 241 us; the launch traced here: 240 us
  matrix products  91 us (38%)
  blocking collectives  55.2 us (23%)
  waiting for transfers between devices  35.8 us (15%)
  local copies, waits for them, and re-layouts  19.9 us (8%)
  starting transfers between devices  18.5 us (8%)
  between operations  13.8 us (6%)
  other arithmetic  5.7 us (2%)
    all_gather x2, blocking collectives, device_step(): gathered = lax.all_gather(ffn_in, 'dp', axis=0, tiled=True)  55.2 us
    all_to_all x2, waiting for transfers between devices, device_step(): returned = lax.all_to_all(expert_out, 'dp', 0, 0, tiled=True)  35.6 us
    dot_general x2, matrix products, device_step(): jnp.einsum('nscf,nfd->sncd', hidden, w2_exp[layer_idx], preferred_element...  31.6 us
    dot_general x2, matrix products, device_step(): jnp.einsum('sncd,ndf->nscf', recv_buf, w3_exp[layer_idx], preferred_eleme...  17.6 us
    all_to_all x2, starting transfers between devices, device_step(): recv_buf = lax.all_to_all(send_buf, 'dp', 0, 0, tiled=True)  10.7 us
    dot_general x2, matrix products, local_attention(): jnp.dot(normed, w_q_l, preferred_element_type=jnp.float32)  9.98 us
    squeeze x1, local copies, waits for them, and re-layouts, device_step(): cache[layer_idx]  8.97 us
    dot_general x2, matrix products, local_attention(): jnp.dot(attn, w_o_l, preferred_element_type=jnp.float32)  8.86 us
  transfers between devices with their start and end apart: 6, of which 2 were waited for; matrix products, arithmetic and copies ran while one was open for 26% of the time, Pallas kernels for 0%

commit v1 on v0

v1 whole, which is shorter than its diff:
```python
import functools

import jax
import jax.numpy as jnp
from jax import lax
from jax.experimental import pallas as pl
from jax.experimental.pallas import tpu as pltpu
from jax.sharding import PartitionSpec as P

NORM_EPS = 1e-6
ATT_SCALE = 1.0 / (192.0 ** 0.5)
LATENT = 512
TB = 16
GA = 4
NS = 4
GB = 8
DROPPED = -(1 << 20)
F32 = jnp.float32
BF16 = jnp.bfloat16


def rms_norm(v):
    return v * lax.rsqrt(jnp.mean(v * v, axis=-1, keepdims=True) + NORM_EPS)


def dot(a, b):
    return jnp.dot(a, b, preferred_element_type=F32)


def dot_nt(a, b):
    return lax.dot_general(a, b, (((1,), (1,)), ((), ())), preferred_element_type=F32)


def make_kernel(group, layers, tok, d_model, seq, kv_dim, heads, n_exp, top_k, cap, ff, chunks):
    chips = group // 2
    rows_e = group * cap
    n_rows = n_exp * rows_e
    n_tok = group * tok
    n_bg = tok // TB
    n_a = n_exp // GA
    n_b = n_exp // GB
    pair = 2 * kv_dim

    def kernel(x_ref, len_ref, tab_ref, w1s_ref, w3s_ref, w2s_ref, cache_hbm, wq_hbm, wo_hbm, w1_hbm, w3_hbm, w2_hbm,
               out_ref,
               wqb, wob, kvb, w1b, w3b, w2b, xres, qs, os, g_all, tabs, disp, comb, xd, hid, hsb, pf,
               psend, prx, fsend, frx, n1send, n1rx, n2send, n2rx,
               wq_sem, kv_sem, wo_sem, w13_sem, w2_sem, tab_s, tab_r, ag_s, ag_r, rs_s, rs_r):
        me = lax.axis_index("dp")
        c = lax.rem(me, 2)
        xx = me // 2
        fwd_chip = lax.rem(xx + 1 + 2 * c, chips)
        bwd_chip = lax.rem(xx + 3 - 2 * c, chips)
        far_chip = lax.rem(xx + 2, chips)
        fwd = 2 * fwd_chip + c
        bwd = 2 * bwd_chip + c
        far = 2 * far_chip + c
        partner = 2 * xx + 1 - c

        def wq_copy(l, p):
            return pltpu.make_async_copy(wq_hbm.at[l, :, pl.ds(p * pair, pair)], wqb.at[:, pl.ds(p * pair, pair)], wq_sem.at[p])

        def kv_copy(l, b):
            return pltpu.make_async_copy(cache_hbm.at[l, pl.ds(b * TB, TB)], kvb.at[pl.ds(b * TB, TB)], kv_sem.at[b])

        def wo_copy(l):
            return pltpu.make_async_copy(wo_hbm.at[l], wob, wo_sem)

        def w13_copies(l, i):
            slot = lax.rem(i, NS)
            return (pltpu.make_async_copy(w1_hbm.at[l, pl.ds(i * GA, GA)], w1b.at[slot], w13_sem.at[0, slot]),
                    pltpu.make_async_copy(w3_hbm.at[l, pl.ds(i * GA, GA)], w3b.at[slot], w13_sem.at[1, slot]))

        def w2_copy(l, k, i):
            c0, cw = chunks[k]
            return pltpu.make_async_copy(w2_hbm.at[l, pl.ds(i * GB, GB), :, pl.ds(c0, cw)],
                                         w2b.at[i, :, :, pl.ds(0, cw)], w2_sem.at[i])

        def start_attn(l):
            for p in range(heads // 2):
                wq_copy(l, p).start()
            for b in range(n_bg):
                kv_copy(l, b).start()
            wo_copy(l).start()

        def start_w13(l, i):
            for cp in w13_copies(l, i):
                cp.start()

        start_attn(0)

        barrier = pltpu.get_barrier_semaphore()
        for o in range(1, group):
            pl.semaphore_signal(barrier, inc=1, device_id={"dp": lax.rem(me + o, group)}, device_id_type=pl.DeviceIdType.MESH)
        pl.semaphore_wait(barrier, group - 1)

        def remote(src, dst, s_sem, r_sem, dev):
            return pltpu.make_async_remote_copy(src_ref=src, dst_ref=dst, send_sem=s_sem, recv_sem=r_sem,
                                                device_id={"dp": dev}, device_id_type=pl.DeviceIdType.MESH)

        tab_cps = []
        for o in range(1, group):
            cp = remote(tab_ref, tabs.at[me], tab_s.at[o - 1], tab_r.at[o - 1], lax.rem(me + o, group))
            cp.start()
            tab_cps.append(cp)
        tabs[me] = tab_ref[...]

        pending_sends = list(tab_cps)

        for l in range(layers):
            x_in = x_ref[...] if l == 0 else xres[...]
            h = rms_norm(x_in.astype(F32)).astype(BF16)
            for p in range(heads // 2):
                wq_copy(l, p).wait()
                qp = dot(h, wqb[:, p * pair:(p + 1) * pair])
                lo = (kv_dim // 128) * 128
                odd = pltpu.roll(qp[:, lo:], pair - kv_dim, 1)[:, :kv_dim].astype(BF16)
                even = qp[:, :kv_dim].astype(BF16)
                for b in range(n_bg):
                    qs[b, (2 * p) * TB:(2 * p + 1) * TB, :] = even[b * TB:(b + 1) * TB]
                    qs[b, (2 * p + 1) * TB:(2 * p + 2) * TB, :] = odd[b * TB:(b + 1) * TB]
            if l == 0:
                for i in range(2):
                    start_w13(0, i)
            for b in range(n_bg):
                kv_copy(l, b).wait()
            cols = TB * seq
            row_i = lax.broadcasted_iota(jnp.int32, (heads * TB, cols), 0)
            col_i = lax.broadcasted_iota(jnp.int32, (heads * TB, cols), 1)
            own = lax.rem(row_i, TB) == col_i // seq
            lane = lax.broadcasted_iota(jnp.int32, (1, cols), 1)
            for b in range(n_bg):
                lim = jnp.zeros((1, cols), jnp.int32)
                for i in range(TB):
                    lim = jnp.where(lane // seq == i, len_ref[b * TB + i], lim)
                in_len = lax.rem(lane, seq) < lim
                keys = kvb[b * TB:(b + 1) * TB].reshape(cols, kv_dim)
                s = dot_nt(qs[b], keys) * ATT_SCALE
                s = jnp.where(jnp.logical_and(own, in_len), s, -jnp.inf)
                e = jnp.exp(s - jnp.max(s, axis=-1, keepdims=True))
                pr = (e * (1.0 / jnp.sum(e, axis=-1, keepdims=True))).astype(BF16)
                vals = kvb[b * TB:(b + 1) * TB, :, :LATENT].reshape(cols, LATENT)
                o_blk = dot(pr, vals).astype(BF16)
                for hh in range(heads):
                    os[b * TB:(b + 1) * TB, hh * LATENT:(hh + 1) * LATENT] = o_blk[hh * TB:(hh + 1) * TB]
            if l == 0:
                for i in range(2, NS):
                    start_w13(0, i)
                for i in range(n_b):
                    w2_copy(0, 0, i).start()
            wo_copy(l).wait()
            x1 = (x_in.astype(F32) + dot(os[...], wob[...])).astype(BF16)
            xres[...] = x1
            g_all[l, me] = rms_norm(x1.astype(F32)).astype(BF16)

            def ag(k, blk, dev):
                cp = remote(g_all.at[l, blk], g_all.at[l, blk], ag_s.at[l, k], ag_r.at[l, k], dev)
                cp.start()
                pending_sends.append(cp)
                return cp

            cp_a = ag(0, me, fwd)
            cp_b = ag(1, me, bwd)
            cp_d0 = ag(2, me, partner)

            if l == 0:
                for cp in tab_cps:
                    cp.wait_recv()
            base = (me * n_rows).astype(F32)
            half = lax.broadcasted_iota(jnp.int32, (2 * top_k, 2 * tok), 1) < tok
            tiles = []
            for ch in range(chips):
                t = jnp.where(half, tabs[2 * ch, 2 * top_k * l:2 * top_k * (l + 1)],
                              tabs[2 * ch + 1, 2 * top_k * l:2 * top_k * (l + 1)])
                tiles.append(t)
            codes = [(t[:top_k] - base).astype(jnp.int32) for t in tiles]
            codes = jnp.concatenate(codes, axis=1)

            def build_disp(i, _):
                r0 = pl.multiple_of(i * 32, 32)
                ri = lax.broadcasted_iota(jnp.int32, (32, n_tok), 0) + r0
                hit = jnp.zeros((32, n_tok), F32)
                for j in range(top_k):
                    hit = jnp.where(ri == codes[j:j + 1, :], 1.0, hit)
                disp[pl.ds(r0, 32), :] = hit.astype(BF16)
                return 0

            lax.fori_loop(0, n_rows // 32, build_disp, 0)
            for ch in range(chips):
                tt = tiles[ch].T
                tcode = (tt[:, :top_k] - base).astype(jnp.int32)
                tw = tt[:, top_k:2 * top_k]
                for rb in range(n_rows // 128):
                    ri = lax.broadcasted_iota(jnp.int32, (2 * tok, 128), 1) + rb * 128
                    w = jnp.zeros((2 * tok, 128), F32)
                    for j in range(top_k):
                        w = jnp.where(ri == tcode[:, j:j + 1], tw[:, j:j + 1], w)
                    w_hi = w.astype(BF16)
                    rem1 = w - w_hi.astype(F32)
                    w_mid = rem1.astype(BF16)
                    w_lo = (rem1 - w_mid.astype(F32)).astype(BF16)
                    sl = slice(rb * 128, (rb + 1) * 128)
                    comb[ch, 0:2 * tok, sl] = w_hi
                    comb[ch, 2 * tok:4 * tok, sl] = w_mid
                    comb[ch, 4 * tok:6 * tok, sl] = w_lo

            cp_a.wait_recv()
            cp_f = ag(3, bwd, fwd)
            cp_d1 = ag(4, bwd, partner)
            cp_b.wait_recv()
            cp_d2 = ag(5, fwd, partner)
            cp_f.wait_recv()
            cp_d3 = ag(6, far, partner)
            for cp in (cp_d0, cp_d1, cp_d2, cp_d3):
                cp.wait_recv()

            g_mat = g_all[l].reshape(n_tok, d_model)
            s_gate = dot_nt(g_mat, w3s_ref[l])
            s_up = dot_nt(g_mat, w1s_ref[l])
            hsb[...] = (s_gate * jax.nn.sigmoid(s_gate) * s_up).astype(BF16)

            def dispatch(i, _):
                r0 = pl.multiple_of(i * 256, 256)
                xd[pl.ds(r0, 256), :] = dot(disp[pl.ds(r0, 256), :], g_all[l].reshape(n_tok, d_model)).astype(BF16)
                return 0

            lax.fori_loop(0, n_rows // 256, dispatch, 0)

            def step_a(i, _):
                slot = lax.rem(i, NS)
                for cp in w13_copies(l, i):
                    cp.wait()
                for k in range(GA):
                    r0 = pl.multiple_of((i * GA + k) * rows_e, rows_e)
                    xe = xd[pl.ds(r0, rows_e), :]
                    gate = dot(xe, w3b[slot, k])
                    up = dot(xe, w1b[slot, k])
                    hid[pl.ds(r0, rows_e), :] = (gate * jax.nn.sigmoid(gate) * up).astype(BF16)

                @pl.when(i + NS < n_a)
                def _():
                    start_w13(l, i + NS)

                if l + 1 < layers:
                    @pl.when(i + NS >= n_a)
                    def _():
                        start_w13(l + 1, i + NS - n_a)
                return 0

            lax.fori_loop(0, n_a, step_a, 0)

            def step_b(k):
                cw = chunks[k][1]

                def body(i, _):
                    w2_copy(l, k, i).wait()
                    for kk in range(GB):
                        r0 = pl.multiple_of((i * GB + kk) * rows_e, rows_e)
                        xd[pl.ds(r0, rows_e), 0:cw] = dot(hid[pl.ds(r0, rows_e), :], w2b[i, kk, :, 0:cw]).astype(BF16)
                    if k + 1 < len(chunks):
                        w2_copy(l, k + 1, i).start()
                    elif l + 1 < layers:
                        w2_copy(l + 1, 0, i).start()
                    return 0

                return body

            def combine(k):
                c0, cw = chunks[k]
                cs = slice(c0, c0 + cw)
                for ch in range(chips):
                    r = dot(comb[ch], xd[:, 0:cw])
                    sh = dot(hsb[ch * 2 * tok:(ch + 1) * 2 * tok, :], w2s_ref[l, :, cs])
                    r = sh + (r[0:2 * tok] + r[2 * tok:4 * tok] + r[4 * tok:6 * tok])
                    pf[2 * ch, :, cs] = r[:tok]
                    pf[2 * ch + 1, :, cs] = r[tok:]

            def rs(k, j, src, dst, dev):
                cp = remote(src, dst, rs_s.at[l, k, j], rs_r.at[l, k, j], dev)
                cp.start()
                pending_sends.append(cp)
                return cp

            def rs_pair(k):
                ds = pl.ds(*chunks[k])
                for ch in range(chips):
                    psend[l, ch, :, ds] = pf[2 * ch + 1 - c, :, ds].astype(BF16)
                return rs(k, 0, psend.at[l, :, :, ds], prx.at[l, :, :, ds], partner)

            def chip_sum(k, chip):
                ds = pl.ds(*chunks[k])
                return pf[2 * chip + c, :, ds] + prx[l, chip, :, ds].astype(F32)

            def rs_far(k, cp):
                ds = pl.ds(*chunks[k])
                cp.wait_recv()
                fsend[l, :, ds] = chip_sum(k, far_chip).astype(BF16)
                cp_far = rs(k, 1, fsend.at[l, :, ds], frx.at[l, :, ds], fwd)
                n1send[l, :, ds] = chip_sum(k, bwd_chip).astype(BF16)
                cp_n1 = rs(k, 2, n1send.at[l, :, ds], n1rx.at[l, :, ds], bwd)
                return cp_far, cp_n1

            def rs_near(k, cp_far):
                ds = pl.ds(*chunks[k])
                cp_far.wait_recv()
                n2send[l, :, ds] = (chip_sum(k, fwd_chip) + frx[l, :, ds].astype(F32)).astype(BF16)
                return rs(k, 3, n2send.at[l, :, ds], n2rx.at[l, :, ds], fwd)

            def rs_final(k, cp_n1, cp_n2):
                ds = pl.ds(*chunks[k])
                cp_n1.wait_recv()
                cp_n2.wait_recv()
                tot = (xres[:, ds].astype(F32) + chip_sum(k, xx) + n1rx[l, :, ds].astype(F32)
                       + n2rx[l, :, ds].astype(F32))
                return tot.astype(BF16)

            if l + 1 < layers:
                start_attn(l + 1)
            lax.fori_loop(0, n_b, step_b(0), 0)
            combine(0)
            cp_p0 = rs_pair(0)
            lax.fori_loop(0, n_b // 2, step_b(1), 0)
            cp_far0, cp_n10 = rs_far(0, cp_p0)
            lax.fori_loop(n_b // 2, n_b, step_b(1), 0)
            combine(1)
            cp_p1 = rs_pair(1)
            cp_n20 = rs_near(0, cp_far0)
            cp_far1, cp_n11 = rs_far(1, cp_p1)
            y0 = rs_final(0, cp_n10, cp_n20)
            cp_n21 = rs_near(1, cp_far1)
            y1 = rs_final(1, cp_n11, cp_n21)
            dst = out_ref if l + 1 == layers else xres
            dst[:, chunks[0][0]:chunks[0][0] + chunks[0][1]] = y0
            dst[:, chunks[1][0]:chunks[1][0] + chunks[1][1]] = y1

        for cp in pending_sends:
            cp.wait_send()

    vm = pltpu.VMEM
    cmax = max(cw for _, cw in chunks)
    nk = len(chunks)
    dma = pltpu.SemaphoreType.DMA
    scratch = [
        vm((d_model, heads * kv_dim), BF16), vm((heads * LATENT, d_model), BF16), vm((tok, seq, kv_dim), BF16),
        vm((NS, GA, d_model, ff), BF16), vm((NS, GA, d_model, ff), BF16), vm((n_b, GB, ff, cmax), BF16),
        vm((tok, d_model), BF16), vm((n_bg, heads * TB, kv_dim), BF16), vm((tok, heads * LATENT), BF16),
        vm((layers, group, tok, d_model), BF16), vm((group, layers * 2 * top_k, 2 * tok), F32),
        vm((n_rows, n_tok), BF16), vm((chips, 6 * tok, n_rows), BF16),
        vm((n_rows, d_model), BF16), vm((n_rows, ff), BF16),
        vm((n_tok, ff // group), BF16), vm((group, tok, d_model), F32),
        vm((layers, chips, tok, d_model), BF16), vm((layers, chips, tok, d_model), BF16),
        vm((layers, tok, d_model), BF16), vm((layers, tok, d_model), BF16),
        vm((layers, tok, d_model), BF16), vm((layers, tok, d_model), BF16),
        vm((layers, tok, d_model), BF16), vm((layers, tok, d_model), BF16),
        dma((heads // 2,)), dma((n_bg,)), dma, dma((2, NS)), dma((n_b,)),
        dma((group - 1,)), dma((group - 1,)), dma((layers, 7)), dma((layers, 7)),
        dma((layers, nk, 4)), dma((layers, nk, 4)),
    ]
    return kernel, scratch


def solution(mesh):
    group = mesh.shape['dp']
    tok_axes = ('replica', 'dp')
    in_specs = (
        P(tok_axes, None), P(tok_axes), P(None, tok_axes, None, None),
        P(None, None, None), P(None, None, None),
        P(None, tok_axes, None), P(None, tok_axes, None), P(None, tok_axes, None),
        P(None, 'dp', None, None), P(None, 'dp', None, None), P(None, 'dp', None, None),
        P(None, None, 'dp'), P(None, None, 'dp'), P(None, 'dp', None),
    )

    def device_step(x, lengths, cache, w_q, w_o, expert_ids, slots, route_w, w1_exp, w3_exp, w2_exp, w1_sh, w3_sh, w2_sh):
        tok, d_model = x.shape
        layers, _, seq, kv_dim = cache.shape
        heads = w_q.shape[2] // kv_dim
        n_exp, ff = w1_exp.shape[1], w1_exp.shape[3]
        top_k = expert_ids.shape[2]
        cap = max(1, (2 * tok * top_k) // (n_exp * group))
        me = lax.axis_index('dp')
        rows_e = group * cap
        code = jnp.where(slots >= 0, expert_ids * rows_e + me * cap + slots, DROPPED).astype(F32)
        tab = jnp.concatenate([code.transpose(0, 2, 1), route_w.transpose(0, 2, 1)], axis=1)
        tab = jnp.concatenate([tab, tab], axis=2).reshape(layers * 2 * top_k, 2 * tok)
        chunks = ((0, 512), (512, d_model - 512))
        kernel, scratch = make_kernel(group, layers, tok, d_model, seq, kv_dim, heads, n_exp, top_k, cap, ff, chunks)
        vmem = pl.BlockSpec(memory_space=pltpu.VMEM)
        hbm = pl.BlockSpec(memory_space=pl.ANY)
        return pl.pallas_call(
            kernel,
            name='mla_moe_decode',
            out_shape=jax.ShapeDtypeStruct((tok, d_model), BF16),
            in_specs=[vmem, pl.BlockSpec(memory_space=pltpu.SMEM), vmem, vmem, vmem, vmem] + [hbm] * 6,
            out_specs=vmem,
            scratch_shapes=scratch,
            compiler_params=pltpu.CompilerParams(collective_id=0, has_side_effects=True, vmem_limit_bytes=67043328),
        )(x, lengths, tab, w1_sh.transpose(0, 2, 1), w3_sh.transpose(0, 2, 1), w2_sh,
          cache, w_q, w_o, w1_exp, w3_exp, w2_exp)

    return jax.shard_map(device_step, mesh=mesh, in_specs=in_specs, out_specs=P(tok_axes, None), check_vma=False)
```

time: 241 us -> 108 us (0.45)
  Pallas kernels: 0 us -> 103 us
  matrix products: 91 us -> 0 us
  blocking collectives: 55.2 us -> 0 us
  waiting for transfers between devices: 35.8 us -> 0 us
  starting transfers between devices: 18.5 us -> 0 us
  local copies, waits for them, and re-layouts: 19.9 us -> 1.55 us
  between operations: 13.8 us -> 0.01 us
  other arithmetic: 5.7 us -> 2.17 us
    pallas_call x0 -> x1, Pallas kernels: none -> 103 us  [device_step(): pl.pallas_call(kernel, name='mla_moe_decode', out_shape=jax.ShapeDtypeStr...]
    dot_general x18 -> x0, matrix products: 82.2 us -> none  [the longest x2 31.6 us: device_step(): jnp.einsum('nscf,nfd->sncd', hidden, w2_exp[layer_idx], preferred_element...]
    all_gather x2 -> x0, blocking collectives: 55.2 us -> none  [device_step(): gathered = lax.all_gather(ffn_in, 'dp', axis=0, tiled=True)]
    all_to_all x4 -> x0, waiting for transfers between devices: 35.6 us -> none  [the longest x2 35.6 us: device_step(): returned = lax.all_to_all(expert_out, 'dp', 0, 0, tiled=True)]
    all_to_all x4 -> x0, starting transfers between devices: 18.5 us -> none  [the longest x2 10.7 us: device_step(): recv_buf = lax.all_to_all(send_buf, 'dp', 0, 0, tiled=True)]
    squeeze x1 -> x0, local copies, waits for them, and re-layouts: 8.97 us -> none  [device_step(): cache[layer_idx]]
    sub x2 -> x0, matrix products: 8.77 us -> none  [local_attention(): jax.nn.softmax(jnp.where(valid, scores, -jnp.inf), axis=-1)]
    reshape x6 -> x0, local copies, waits for them, and re-layouts: 4.95 us -> none  [the longest x2 2.85 us: device_step(): send_buf = send_buf.reshape(group, local_experts, capacity, d_model)]
  transfers between devices with their start and end apart: 6 -> 0, of which waited for: 2 -> 0; matrix products, arithmetic and copies ran while one was open for 26% -> 0% of each run, Pallas kernels for 0% -> 0%
where the time goes in v1:
time: 108 us; the launch traced here: 107 us
  Pallas kernels  103 us (95%)
  other arithmetic  2.17 us (2%)
  local copies, waits for them, and re-layouts  1.55 us (1%)
    pallas_call x1, Pallas kernels, device_step(): pl.pallas_call(kernel, name='mla_moe_decode', out_shape=jax.ShapeDtypeStr...  103 us

profile of v1, /device:TPU:81, one launch (start us, length us, event | category | flops | bytes accessed | tf_op | source)
XLA Modules:
  0.0 106.7 jit_solution(17610158710931914713)
XLA Ops:
  0.0 0.7 convert_bitcast_fusion
  0.7 1.5 %maximum_maximum_fusion = f32[2,16,128]{2,1,0:T(8,128)} fusion(f32[2,8,64]{2,1,0:T(8,128)} %bitcast.9, f32[2,8,64]{2,1,0:T(8,128)S(1)} %convert_bitcast_fusion), kind=kLoop, calls=%fused_computation | loop fusion | flops 12288 | bytes 24576 | tf_op jit(solution)/shard_map/concatenate | solution.py:384
  2.2 102.9 %mla_moe_decode.1 = bf16[64,896]{1,0:T(8,128)(2,1)} custom-call(bf16[64,896]{1,0:T(8,128)(2,1)} %x_ref.1, s32[64]{0:T(128)} %len_ref.1, f32[32,128]{1,0:T(8,128)} %bitcast.8, bf16[2,32,896]{2,1,0:T(8,128)(2,1)} %bitcast.6, bf16[2,32,896]{2,1,0:T(8,128)(2,1)} %bitcast.7, bf16[2,32,896]{2,1,0:T(8,128)(2,1)} %w2s_ref.1, bf16[2,64,64,576]{3,2,1,0:T(8,128)(2,1)} %cache_hbm.1, ...), custom_call_target="tpu_custom_call" | custom-call | tf_op jit(solution)/shard_map/mla_moe_decode/pallas_call | solution.py:389
  105.1 1.6 %copy.16 = bf16[64,896]{1,0:T(8,128)(2,1)} copy(bf16[64,896]{1,0:T(8,128)(2,1)} %mla_moe_decode.1) | data formatting | bytes 229376
